TPU v7x, 8 devices: a whole 2x2x1 slice. The times are simulated.
8 devices in a mesh: graph: 8 (over z, y, x, core).
Axes of the slice: x: 2, y: 2, z: 1, core: 2. Of those that a mesh axis runs over, the one named last changes fastest.
Arguments:
- feats: bfloat16 [8192, 602], P('graph')
- w_one: float32 [602, 256], replicated
- w_two: float32 [256, 41], replicated
- send_idx: int32 [64, 64], P('graph')
- send_count: int32 [64], P('graph')
- edge_src: int32 [8192, 16], P('graph')
- edge_wt: float32 [8192, 16], P('graph')
- labels: int32 [8192], P('graph')
- label_mask: int32 [8192], P('graph')
Outputs:
- output 1: float32 [], replicated
- output 2: float32 [602, 256], replicated
- output 3: float32 [256, 41], replicated
All inputs are finite; a program needn't handle non-finite values.
Results may differ from a plain program's by a relative error of at most 0.00226.
Values are sent between devices in bfloat16 or wider.
A program may use at most 1 GiB of HBM per device.

v0:
```python
import jax
import jax.numpy as jnp
from jax import lax
from jax.sharding import PartitionSpec as P


def solution(mesh):
    dev_count = mesh.shape["graph"]

    def device_step(feats, w_one, w_two, send_idx, send_count, edge_src, edge_wt, labels, label_mask):
        row_count = feats.shape[0]
        halo_rows = send_idx.shape[1]
        in_deg = edge_src.shape[1]
        list_ids = send_idx.reshape(dev_count * halo_rows)
        list_ok = (jnp.arange(halo_rows)[None, :] < send_count[:, None]).reshape(dev_count * halo_rows, 1)
        flat_src = edge_src.reshape(row_count * in_deg)
        w_one_b = w_one.astype(jnp.bfloat16)
        w_two_b = w_two.astype(jnp.bfloat16)

        def aggregate(h_rows):
            outgoing = jnp.where(list_ok, h_rows[list_ids], 0)
            incoming = lax.all_to_all(outgoing, "graph", 0, 0, tiled=True)
            ext_rows = jnp.concatenate([h_rows, incoming], axis=0)
            return jnp.sum(ext_rows[edge_src].astype(jnp.float32) * edge_wt[:, :, None], axis=1)

        z_one = aggregate(feats).astype(jnp.bfloat16)
        h_one = jnp.maximum(jnp.dot(z_one, w_one_b, preferred_element_type=jnp.float32), 0.0).astype(jnp.bfloat16)
        z_two = aggregate(h_one).astype(jnp.bfloat16)
        logits = jnp.dot(z_two, w_two_b, preferred_element_type=jnp.float32)
        mask_f = label_mask.astype(jnp.float32)
        label_total = lax.psum(jnp.sum(mask_f), "graph")
        log_prob = jax.nn.log_softmax(logits, axis=-1)
        onehot = (labels[:, None] == jnp.arange(logits.shape[1])[None, :]).astype(jnp.float32)
        loss_val = -lax.psum(jnp.sum(mask_f[:, None] * onehot * log_prob), "graph") / label_total
        d_logits = ((jnp.exp(log_prob) - onehot) * (mask_f / label_total)[:, None]).astype(jnp.bfloat16)
        grad_two = lax.psum(jnp.einsum("nf,nc->fc", z_two, d_logits, preferred_element_type=jnp.float32), "graph")
        d_z2 = jnp.einsum("nc,fc->nf", d_logits, w_two_b, preferred_element_type=jnp.float32)
        contrib = (edge_wt[:, :, None] * d_z2[:, None, :]).reshape(row_count * in_deg, d_z2.shape[1])
        ext_grad = jax.ops.segment_sum(contrib, flat_src, num_segments=row_count + dev_count * halo_rows)
        returned = lax.all_to_all(ext_grad[row_count:], "graph", 0, 0, tiled=True)
        d_h1 = ext_grad[:row_count] + jax.ops.segment_sum(jnp.where(list_ok, returned, 0.0), list_ids, num_segments=row_count)
        d_y1 = jnp.where(h_one > 0, d_h1, 0.0).astype(jnp.bfloat16)
        grad_one = lax.psum(jnp.einsum("nf,nh->fh", z_one, d_y1, preferred_element_type=jnp.float32), "graph")
        return loss_val, grad_one, grad_two

    row_spec = P("graph", None)
    vec_spec = P("graph")
    return jax.shard_map(device_step, mesh=mesh, in_specs=(row_spec, P(), P(), row_spec, vec_spec, row_spec, row_spec, vec_spec, vec_spec), out_specs=(P(), P(), P()), check_vma=False)
```

profile of v0, /device:TPU:0, one launch (start us, length us, event | category | flops | bytes accessed | tf_op | source)
XLA Modules:
  0.0 388.6 jit_solution(4983318761758243891)
XLA Ops:
  7.2 1.7 copy.17
  8.9 0.8 reshape.84
  9.6 0.7 iota_compare_fusion.1
  10.4 2.0 gather_fusion
  12.4 1.0 broadcast_select_fusion
  13.4 4.3 %all-to-all-start = ((bf16[8,64,602]{2,1,0:T(8,128)(2,1)}), bf16[8,64,602]{2,1,0:T(8,128)(2,1)S(1)}, u32[]{:S(2)}, u32[]{:S(2)}) async-start(bf16[8,64,602]{2,1,0:T(8,128)(2,1)} %broadcast_select_fusion), calls=%async_computation | async-start | bytes 1310720 | tf_op jit(solution)/shard_map/all_to_all | solution.py:22
  17.7 0.2 copy.18
  17.9 0.2 reshape.95
  18.1 1.0 copy.19
  19.1 9.7 %all-to-all-done = bf16[8,64,602]{2,1,0:T(8,128)(2,1)S(1)} async-done(((bf16[8,64,602]{2,1,0:T(8,128)(2,1)}), bf16[8,64,602]{2,1,0:T(8,128)(2,1)S(1)}, u32[]{:S(2)}, u32[]{:S(2)}) %all-to-all-start) | async-done | bytes 616480 | tf_op jit(solution)/shard_map/all_to_all | solution.py:22
  28.8 0.8 copy-done.5
  29.7 1.3 pad_maximum_fusion
  31.0 67.3 %gather_fusion.1 = bf16[16384,602]{1,0:T(8,128)(2,1)} fusion(bf16[1536,602]{1,0:T(8,128)(2,1)S(1)} %pad_maximum_fusion, s32[16384]{0:T(1024)S(1)} %broadcast_clamp_fusion), kind=kCustom, calls=%fused_computation.1 | custom fusion | bytes 39518208 | tf_op jit(solution)/shard_map/gather | solution.py:24
  98.3 16.8 %fusion = bf16[1024,602]{1,0:T(8,128)(2,1)S(1)} fusion(f32[1024,16]{1,0:T(8,128)S(1)} %copy-done, bf16[16384,602]{1,0:T(8,128)(2,1)} %gather_fusion.1), kind=kLoop, calls=%fused_computation.7 | loop fusion | flops 28973056 | bytes 21024768 | tf_op jit(solution)/shard_map/reduce_sum | solution.py:24
  115.1 0.6 fusion.2
  115.7 2.0 gather_fusion.2
  117.7 0.8 broadcast_select_fusion.1
  118.5 2.1 all-to-all-start.1
  120.7 0.6 convert_reduce_fusion
  121.3 24.0 %psum.29 = f32[]{:T(128)} all-reduce(f32[]{:T(128)} %convert_reduce_fusion), channel_id=1, replica_groups=mesh['graph'=8] {'graph'}, use_global_device_ids=true, to_apply=%region_7.8 | all-reduce | flops 1 | bytes 8 | tf_op jit(solution)/shard_map/psum | solution.py:31
  145.3 0.2 mul.60
  145.5 0.2 copy.21
  145.7 0.2 reshape.119
  145.9 0.7 broadcast_divide_fusion
  146.6 0.1 pad_maximum_fusion.1
  146.7 64.8 %gather_fusion.3 = bf16[16384,256]{1,0:T(8,128)(2,1)} fusion(bf16[1536,256]{1,0:T(8,128)(2,1)S(1)} %pad_maximum_fusion.1, s32[16384]{0:T(1024)S(1)} %broadcast_clamp_fusion), kind=kCustom, calls=%fused_computation.3 | custom fusion | bytes 16842752 | tf_op jit(solution)/shard_map/gather | solution.py:24
  211.5 7.6 %fusion.1 = bf16[1024,256]{1,0:T(8,128)(2,1)S(1)} fusion(f32[1024,16]{1,0:T(8,128)S(1)} %copy-done.1, bf16[16384,256]{1,0:T(8,128)(2,1)} %gather_fusion.3), kind=kLoop, calls=%fused_computation.9 | loop fusion | flops 12320768 | bytes 8978432 | tf_op jit(solution)/shard_map/reduce_sum | solution.py:24
  219.1 0.3 fusion.20
  219.4 0.3 fusion.15
  219.8 0.1 copy-done.4
  219.9 6.4 %bitcast_multiply_fusion = f32[16384,256]{1,0:T(8,128)} fusion(f32[1024,256]{1,0:T(8,128)S(1)} %fusion.15, f32[16384]{0:T(1024)S(1)} %mul.60), kind=kLoop, calls=%fused_computation.10 | loop fusion | flops 4194304 | bytes 17891328 | tf_op jit(solution)/shard_map/mul | solution.py:38
  226.3 88.5 %scatter_custom_fusion = f32[1536,256]{1,0:T(8,128)S(1)} fusion(s32[16384]{0:T(1024)S(1)} %reshape.119, f32[16384,256]{1,0:T(8,128)} %bitcast_multiply_fusion, f32[]{:T(128)} %constant.6.clone.1), kind=kCustom, calls=%fused_computation.16 | custom fusion | flops 4194304 | bytes 1573376 | tf_op jit(solution)/shard_map/scatter-add | solution.py:39
  314.8 0.8 slice.17
  315.6 2.9 all-to-all-start.2
  318.5 0.0 all-reduce.3.cloned.1.call-start
  318.6 0.1 lt.41
  318.7 0.1 reshape.127
  318.7 0.1 slice.16
  318.8 9.3 %all-to-all-done.2 = f32[8,64,256]{2,1,0:T(8,128)} async-done(((f32[8,64,256]{2,1,0:T(8,128)}), f32[8,64,256]{2,1,0:T(8,128)}, u32[]{:S(2)}, u32[]{:S(2)}) %all-to-all-start.2) | async-done | bytes 524320 | tf_op jit(solution)/shard_map/all_to_all | solution.py:40
  328.1 2.0 bitcast_select_fusion
  330.0 4.3 %scatter_fusion = f32[1024,256]{1,0:T(8,128)S(1)} fusion(f32[1024,256]{1,0:T(8,128)S(1)} %slice.16, s32[512]{0:T(512)S(1)} %reshape.127, f32[512,256]{1,0:T(8,128)} %bitcast_select_fusion), kind=kCustom, calls=%fused_computation.5 | custom fusion | flops 131072 | bytes 1574912 | tf_op jit(solution)/shard_map/scatter-add | solution.py:41
  334.4 1.4 fusion.5
  335.7 0.0 all-reduce.3.cloned.1.call-update
  335.8 1.3 fusion.11
  337.0 0.7 multiply_reduce_fusion
  337.7 23.3 %all-reduce = (f32[]{:T(128)}, f32[256,41]{0,1:T(8,128)}) all-reduce(f32[]{:T(128)} %multiply_reduce_fusion, f32[256,41]{0,1:T(8,128)S(1)} %fusion.11), channel_id=1, replica_groups=mesh['graph'=8] {'graph'}, use_global_device_ids=true, to_apply=%region_5.6 | all-reduce | flops 10497 | bytes 83976 | tf_op jit(solution)/shard_map/psum | solution.py:34
  362.3 16.3 %all-reduce.3.cloned.1.call-done = f32[602,256]{1,0:T(8,128)} async-done(((f32[602,256]{1,0:T(8,128)}), f32[602,256]{1,0:T(8,128)}) %all-reduce.3.cloned.1.call-update) | async-done | bytes 616464 | tf_op jit(solution)/shard_map/psum | solution.py:43
  378.6 1.9 copy.25
  (32 shorter events, 0.1 us)
Async XLA Ops:
  10.4 7.3 %copy-start.7 = (s32[1024,16]{0,1:T(8,128)S(1)}, s32[1024,16]{0,1:T(8,128)}, u32[]{:S(2)}) copy-start(s32[1024,16]{0,1:T(8,128)} %param.14) | copy-start | bytes 196612
  10.4 7.8 %copy-start.9 = (f32[1024,16]{0,1:T(8,128)S(1)}, f32[1024,16]{0,1:T(8,128)}, u32[]{:S(2)}) copy-start(f32[1024,16]{0,1:T(8,128)} %param.15) | copy-start | bytes 196612
  13.4 15.4 %all-to-all-start = ((bf16[8,64,602]{2,1,0:T(8,128)(2,1)}), bf16[8,64,602]{2,1,0:T(8,128)(2,1)S(1)}, u32[]{:S(2)}, u32[]{:S(2)}) async-start(bf16[8,64,602]{2,1,0:T(8,128)(2,1)} %broadcast_select_fusion), calls=%async_computation | async-start | bytes 1310720 | tf_op jit(solution)/shard_map/all_to_all | solution.py:22
  28.8 0.8 copy-start.5
  30.9 67.4 %copy-start = (f32[1024,16]{1,0:T(8,128)S(1)}, f32[1024,16]{1,0:T(8,128)}, u32[]{:S(2)}) copy-start(f32[1024,16]{1,0:T(8,128)} %copy.19) | copy-start | bytes 196612
  98.3 16.8 %copy-start.6 = (f32[602,256]{1,0:T(8,128)S(1)}, f32[602,256]{1,0:T(8,128)}, u32[]{:S(2)}) copy-start(f32[602,256]{1,0:T(8,128)} %param.10) | copy-start | bytes 1849348
  115.1 31.4 %copy-start.2 = (bf16[1024,602]{1,0:T(8,128)(2,1)}, bf16[1024,602]{1,0:T(8,128)(2,1)S(1)}, u32[]{:S(2)}) copy-start(bf16[1024,602]{1,0:T(8,128)(2,1)S(1)} %fusion) | copy-start | bytes 3698692
  115.1 5.5 %copy-start.11 = (s32[1024]{0:T(1024)S(1)}, s32[1024]{0:T(1024)}, u32[]{:S(2)}) copy-start(s32[1024]{0:T(1024)} %param.17) | copy-start | bytes 12292
  118.5 28.0 %all-to-all-start.1 = ((bf16[8,64,256]{2,1,0:T(8,128)(2,1)}), bf16[8,64,256]{2,1,0:T(8,128)(2,1)S(1)}, u32[]{:S(2)}, u32[]{:S(2)}) async-start(bf16[8,64,256]{2,1,0:T(8,128)(2,1)} %broadcast_select_fusion.1), calls=%async_computation.1 | async-start | bytes 524288 | tf_op jit(solution)/shard_map/all_to_all | solution.py:22
  146.6 64.9 %copy-start.1 = (f32[1024,16]{1,0:T(8,128)S(1)}, f32[1024,16]{1,0:T(8,128)}, u32[]{:S(2)}) copy-start(f32[1024,16]{1,0:T(8,128)} %copy.19) | copy-start | bytes 196612
  211.5 7.6 %copy-start.8 = (f32[256,41]{0,1:T(8,128)S(1)}, f32[256,41]{0,1:T(8,128)}, u32[]{:S(2)}) copy-start(f32[256,41]{0,1:T(8,128)} %param.11) | copy-start | bytes 125956
  211.5 7.9 %copy-start.10 = (s32[1024]{0:T(1024)S(1)}, s32[1024]{0:T(1024)}, u32[]{:S(2)}) copy-start(s32[1024]{0:T(1024)} %param.16) | copy-start | bytes 12292
  219.1 0.8 copy-start.4
  219.9 98.7 %copy-start.12 = (s32[8,64]{1,0:T(8,128)S(1)}, s32[8,64]{1,0:T(8,128)}, u32[]{:S(2)}) copy-start(s32[8,64]{1,0:T(8,128)} %param.12) | copy-start | bytes 6148
  315.6 12.4 %all-to-all-start.2 = ((f32[8,64,256]{2,1,0:T(8,128)}), f32[8,64,256]{2,1,0:T(8,128)}, u32[]{:S(2)}, u32[]{:S(2)}) async-start(f32[8,64,256]{2,1,0:T(8,128)} %bitcast.8), calls=%async_computation.2 | async-start | bytes 1048576 | tf_op jit(solution)/shard_map/all_to_all | solution.py:40
  318.5 60.1 %all-reduce.3.cloned.1.call-start = ((), (), s32[]{:S(2)}) async-start(), calls=%async_computation.3 | async-start | bytes 1245184 | tf_op jit(solution)/shard_map/psum | solution.py:43
  330.0 4.3 %copy-start.3 = (bf16[1024,602]{1,0:T(8,128)(2,1)S(1)}, bf16[1024,602]{1,0:T(8,128)(2,1)}, u32[]{:S(2)}) copy-start(bf16[1024,602]{1,0:T(8,128)(2,1)} %copy-done.2) | copy-start | bytes 3698692
Sparse Core Ops, SparseCore 0:
  335.9 42.7 all-reduce.2
where the time goes:
time: 390 us; the launch traced here: 389 us
  local copies, waits for them, and re-layouts  145 us (37%)
  other arithmetic  131 us (34%)
  blocking collectives  47.2 us (12%)
  waiting for transfers between devices  35.3 us (9%)
  between operations  16.8 us (4%)
  starting transfers between devices  9.37 us (2%)
    gather x2, local copies, waits for them, and re-layouts, aggregate(): ext_rows[edge_src].astype(jnp.float32) * edge_wt[:, :, None]  132 us
    scatter-add x1, other arithmetic, device_step(): jax.ops.segment_sum(contrib, flat_src, num_segments=row_count + dev_count...  88.5 us
    reduce_sum x2, other arithmetic, aggregate(): jnp.sum(ext_rows[edge_src].astype(jnp.float32) * edge_wt[:, :, None], axi...  24.4 us
    psum x1, blocking collectives, device_step(): label_total = lax.psum(jnp.sum(mask_f), 'graph')  24 us
    psum x1, blocking collectives, device_step(): lax.psum(jnp.sum(mask_f[:, None] * onehot * log_prob), 'graph')  23.3 us
    psum x1, waiting for transfers between devices, device_step(): lax.psum(jnp.einsum('nf,nh->fh', z_one, d_y1, preferred_element_type=jnp....  16.3 us
    all_to_all x2, waiting for transfers between devices, aggregate(): incoming = lax.all_to_all(outgoing, 'graph', 0, 0, tiled=True)  9.69 us
    all_to_all x1, waiting for transfers between devices, device_step(): returned = lax.all_to_all(ext_grad[row_count:], 'graph', 0, 0, tiled=True)  9.26 us
  transfers between devices with their start and end apart: 4, of which 3 were waited for; matrix products, arithmetic and copies ran while one was open for 1% of the time, Pallas kernels for 0%

commit v1 on v0

v1 whole, which is shorter than its diff:
```python
import jax
import jax.numpy as jnp
from jax import lax
from jax.experimental import pallas as pl
from jax.experimental.pallas import tpu as pltpu
from jax.sharding import PartitionSpec as P

MESH = pl.DeviceIdType.MESH
F32 = jnp.float32
BF16 = jnp.bfloat16

DEVS = 8
ROWS = 1024
HALO = 64
DEG = 16
EXT = ROWS + DEVS * HALO
FEAT = 602
FEAT_P = 608
FEAT_L = 640
HID = 256
CLS = 41
CLS_P = 48
OUT_SH = 168
LANE = 128
BUILD = 64


def dot_nn(a, b):
    return lax.dot_general(a, b, (((1,), (0,)), ((), ())), preferred_element_type=F32)


def dot_nt(a, b):
    return lax.dot_general(a, b, (((1,), (1,)), ((), ())), preferred_element_type=F32)


def split3(x):
    hi = x.astype(BF16)
    rest = x - hi.astype(F32)
    mid = rest.astype(BF16)
    low = (rest - mid.astype(F32)).astype(BF16)
    return hi, mid, low


def iota(shape, dim):
    return lax.broadcasted_iota(jnp.int32, shape, dim)


def kernel(feats_h, w_one_h, w_two_h, idx_ref, cnt_ref, src_ref, wt_ref, lab_ref, mask_ref,
           loss_ref, g1_ref, g2_ref,
           feats_raw, feats_t, w_one_f, w_two_f, w_two_p, w_one_t, wts, at_hi, at_mid, at_low, sel, sel_t,
           z1_acc, z1_t, h1_t, h1_n, x1, halo1, x2, halo2, th, tret, cnt_src, cnt_in,
           grads, a_in, b_out, b_in, outs,
           in_sem, s1, r1, sc, rc, s2, r2, s3, r3, sa, ra, sb, rb, so, ro, sd, rd):
    me = lax.axis_index("graph")
    core = me % 2
    chip = me // 2
    cx = chip % 2
    cy = chip // 2

    def flip_chip(f):
        fx, fy = f % 2, f // 2
        nx = 1 - cx if fx else cx
        ny = 1 - cy if fy else cy
        return ny * 2 + nx

    def flip_dev(f):
        nc = 1 - core if f % 2 else core
        return flip_chip(f // 2) * 2 + nc

    barrier = pltpu.get_barrier_semaphore()
    for f in range(1, DEVS):
        pl.semaphore_signal(barrier, inc=1, device_id=(flip_dev(f),), device_id_type=MESH)

    in_feats = pltpu.make_async_copy(feats_h, feats_raw, in_sem.at[0])
    in_one = pltpu.make_async_copy(w_one_h, w_one_f, in_sem.at[1])
    in_two = pltpu.make_async_copy(w_two_h, w_two_f, in_sem.at[2])
    in_feats.start()
    in_one.start()
    in_two.start()

    eye = iota((HALO, HALO), 0) == iota((HALO, HALO), 1)
    for q in range(DEVS):
        row = jnp.where(iota((1, HALO), 1) < cnt_ref[q], idx_ref[pl.ds(q, 1), :], -1).astype(F32)
        col = jnp.sum(jnp.where(eye, jnp.broadcast_to(row, (HALO, HALO)), 0.0), axis=1, keepdims=True)
        col = col.astype(jnp.int32)
        hot = iota((HALO, ROWS), 1) == jnp.broadcast_to(col, (HALO, ROWS))
        sel[pl.ds(q * HALO, HALO), :] = jnp.where(hot, 1.0, 0.0).astype(BF16)

    mask_f = mask_ref[...].astype(F32)
    own_count = jnp.sum(mask_f, axis=1, keepdims=True)
    cnt_src[...] = jnp.broadcast_to(own_count, (8, LANE))

    in_feats.wait()
    feats_t[pl.ds(592, FEAT_L - 592), :] = jnp.zeros((FEAT_L - 592, ROWS), BF16)
    feats_t[pl.ds(0, FEAT), :] = feats_raw[...]

    x1[...] = dot_nt(sel[...], feats_t[...]).astype(BF16)

    own_block = pl.ds(pl.multiple_of(me * HALO, HALO), HALO)
    halo1[own_block, :] = jnp.zeros((HALO, FEAT_L), BF16)
    halo2[own_block, :] = jnp.zeros((HALO, HID), BF16)
    tret[own_block, :] = jnp.zeros((HALO, LANE), F32)

    pl.semaphore_wait(barrier, DEVS - 1)

    def exchange(src, dst, send, recv):
        copies = []
        for f in range(1, DEVS):
            peer = flip_dev(f)
            copies.append(pltpu.make_async_remote_copy(
                src_ref=src.at[pl.ds(pl.multiple_of(peer * HALO, HALO), HALO), :],
                dst_ref=dst.at[own_block, :],
                send_sem=send.at[f], recv_sem=recv.at[f],
                device_id=(peer,), device_id_type=MESH))
        return copies

    order = [6, 7, 2, 3, 4, 5, 1]
    ex1 = exchange(x1, halo1, s1, r1)
    for f in order:
        ex1[f - 1].start()
    counts = []
    for f in range(1, DEVS):
        counts.append(pltpu.make_async_remote_copy(
            src_ref=cnt_src, dst_ref=cnt_in.at[f], send_sem=sc.at[f], recv_sem=rc.at[f],
            device_id=(flip_dev(f),), device_id_type=MESH))
        counts[-1].start()

    src = src_ref[...]
    wt = wt_ref[...]
    krow = iota((DEG, ROWS), 0)
    total = wt
    for d in range(1, DEG):
        same = (pltpu.roll(src, d, 0) == src) & (krow >= d)
        total = total + jnp.where(same, pltpu.roll(wt, d, 0), 0.0)
    wts[...] = total

    def build(s_first, s_count):
        def per_lane(t, carry):
            lanes = pl.ds(pl.multiple_of(t * LANE, LANE), LANE)
            src_b = src_ref[:, lanes]
            wt_b = wts[:, lanes]

            def per_rows(b, inner):
                start = pl.multiple_of(s_first + b * BUILD, BUILD)
                rel = src_b - start
                rows = iota((BUILD, LANE), 0)
                acc = jnp.zeros((BUILD, LANE), F32)
                for k in range(DEG):
                    hot = rows == jnp.broadcast_to(rel[k:k + 1, :], (BUILD, LANE))
                    acc = jnp.where(hot, jnp.broadcast_to(wt_b[k:k + 1, :], (BUILD, LANE)), acc)
                hi, mid, low = split3(acc)
                at_hi[pl.ds(start, BUILD), lanes] = hi
                at_mid[pl.ds(start, BUILD), lanes] = mid
                at_low[pl.ds(start, BUILD), lanes] = low
                return inner

            return lax.fori_loop(0, s_count // BUILD, per_rows, carry)

        lax.fori_loop(0, ROWS // LANE, per_lane, 0)

    build(0, ROWS)

    def aggregate(left, first, count, cols):
        rows = pl.ds(first, count)
        return (dot_nn(left, at_hi[rows, cols]) + dot_nn(left, at_mid[rows, cols])
                + dot_nn(left, at_low[rows, cols]))

    def cols_of(t):
        return pl.ds(t * 256, 256)

    for t in range(4):
        z1_acc[:, cols_of(t)] = aggregate(feats_t[pl.ds(0, FEAT_P), :], 0, ROWS, cols_of(t))

    build(ROWS, EXT - ROWS)
    sel_t[...] = sel[...].T

    in_one.wait()
    in_two.wait()
    w_one_t[:, pl.ds(512, FEAT_P - 512)] = jnp.zeros((HID, FEAT_P - 512), BF16)
    w_one_t[:, pl.ds(0, FEAT)] = w_one_f[...].T.astype(BF16)
    w_two_p[...] = jnp.zeros((CLS_P, HID), BF16)
    w_two_p[pl.ds(0, CLS), :] = w_two_f[...].astype(BF16)
    w_two_b = w_two_p[...]

    for f in order:
        ex1[f - 1].wait_recv()
    halo1_t = halo1[...].T[:FEAT_P, :]
    for t in range(4):
        z1_t[:, cols_of(t)] = (z1_acc[:, cols_of(t)]
                               + aggregate(halo1_t, ROWS, EXT - ROWS, cols_of(t))).astype(BF16)

    h1_t[...] = jnp.maximum(dot_nn(w_one_t[...], z1_t[...]), 0.0).astype(BF16)
    x2[...] = dot_nt(sel[...], h1_t[...]).astype(BF16)
    ex2 = exchange(x2, halo2, s2, r2)
    for f in order:
        ex2[f - 1].start()

    h1_n[...] = h1_t[...].T
    z2_acc = aggregate(h1_t[...], 0, ROWS, pl.ds(0, ROWS))
    for f in order:
        ex2[f - 1].wait_recv()
    z2_t = (z2_acc + aggregate(halo2[...].T, ROWS, EXT - ROWS, pl.ds(0, ROWS))).astype(BF16)

    count = cnt_src[...]
    for f in range(1, DEVS):
        counts[f - 1].wait_recv()
        count = count + cnt_in[f]
    count = count[0:1, 0:1]

    logits = dot_nn(w_two_b, z2_t)
    cls_row = iota((CLS_P, ROWS), 0)
    real = cls_row < CLS
    top = jnp.max(jnp.where(real, logits, -3.0e38), axis=0, keepdims=True)
    shifted = logits - top
    expo = jnp.where(real, jnp.exp(shifted), 0.0)
    log_prob = shifted - jnp.log(jnp.sum(expo, axis=0, keepdims=True))
    hit = cls_row == lab_ref[...]
    loss_row = jnp.sum(jnp.where(hit, log_prob, 0.0), axis=0, keepdims=True) * mask_f
    scale = mask_f / count
    d_log = (jnp.exp(log_prob) - jnp.where(hit, 1.0, 0.0)) * scale
    g2_t = jnp.where(real, d_log, 0.0).astype(BF16)
    g2_n = jnp.concatenate([g2_t.astype(F32), jnp.zeros((LANE - CLS_P, ROWS), F32)], axis=0).T.astype(BF16)

    def scatter(first, rows_n):
        rows = pl.ds(first, rows_n)
        return dot_nn(at_hi[rows, :], g2_n) + dot_nn(at_mid[rows, :], g2_n) + dot_nn(at_low[rows, :], g2_n)

    th[...] = scatter(ROWS, EXT - ROWS)
    ex3 = exchange(th, tret, s3, r3)
    for f in order:
        ex3[f - 1].start()

    own_t = scatter(0, ROWS)
    grad_two = dot_nt(g2_t, z2_t)
    loss_sum = jnp.sum(loss_row, axis=1, keepdims=True)
    grad_two = jnp.where(iota((CLS_P, HID), 0) == CLS, jnp.broadcast_to(loss_sum, (CLS_P, HID)), grad_two)
    w_stack = jnp.concatenate(
        [jnp.concatenate([w_two_b.astype(F32), jnp.zeros((LANE - CLS_P, HID), F32)], axis=0)] * 3, axis=0).astype(BF16)

    for f in order:
        ex3[f - 1].wait_recv()
    back = dot_nn(sel_t[...], jnp.concatenate(split3(tret[...]), axis=1))
    own_t = own_t + (back[:, 0:LANE] + back[:, LANE:2 * LANE] + back[:, 2 * LANE:3 * LANE])
    d_h1 = dot_nn(jnp.concatenate(split3(own_t), axis=1), w_stack)
    g1_b = jnp.where(h1_n[...].astype(F32) > 0, d_h1, 0.0).astype(BF16)
    grad_one = dot_nn(z1_t[...], g1_b)

    for h in range(2):
        lanes = slice(h * LANE, (h + 1) * LANE)
        for j in range(3):
            grads[h, j] = grad_one[j * OUT_SH:(j + 1) * OUT_SH, lanes]
        grads[h, 3, pl.ds(0, FEAT_P - 3 * OUT_SH), :] = grad_one[3 * OUT_SH:FEAT_P, lanes]
        grads[h, 3, pl.ds(FEAT_P - 3 * OUT_SH, CLS_P), :] = grad_two[:, lanes]
        grads[h, 3, pl.ds(FEAT_P - 3 * OUT_SH + CLS_P, 16), :] = jnp.zeros((16, LANE), F32)

    mate = flip_dev(1)
    flips = [3, 1, 2]
    copy_a = {}
    for o in flips + [0]:
        to_chip = flip_chip(o)
        copy_a[o] = pltpu.make_async_remote_copy(
            src_ref=grads.at[1 - core, to_chip], dst_ref=a_in.at[o], send_sem=sa.at[o], recv_sem=ra.at[o],
            device_id=(mate,), device_id_type=MESH)
        copy_a[o].start()
    copy_b = {}
    for o in flips:
        to_chip = flip_chip(o)
        copy_a[o].wait_recv()
        b_out[o] = grads[core, to_chip] + a_in[o]
        copy_b[o] = pltpu.make_async_remote_copy(
            src_ref=b_out.at[o], dst_ref=b_in.at[o], send_sem=sb.at[o], recv_sem=rb.at[o],
            device_id=(to_chip * 2 + core,), device_id_type=MESH)
        copy_b[o].start()
    copy_a[0].wait_recv()
    mine = grads[core, chip] + a_in[0]
    for o in flips:
        copy_b[o].wait_recv()
    mine = mine + ((b_in[1] + b_in[2]) + b_in[3])
    outs[core, chip] = mine
    copy_c = {}
    for o in flips:
        copy_c[o] = pltpu.make_async_remote_copy(
            src_ref=outs.at[core, chip], dst_ref=outs.at[core, chip], send_sem=so.at[o], recv_sem=ro.at[o],
            device_id=(flip_chip(o) * 2 + core,), device_id_type=MESH)
        copy_c[o].start()
    copy_d = {}
    for o in [0, 1, 2, 3]:
        at_chip = flip_chip(o)
        if o:
            copy_c[o].wait_recv()
        copy_d[o] = pltpu.make_async_remote_copy(
            src_ref=outs.at[core, at_chip], dst_ref=outs.at[core, at_chip], send_sem=sd.at[o], recv_sem=rd.at[o],
            device_id=(mate,), device_id_type=MESH)
        copy_d[o].start()
    for o in [0, 1, 2, 3]:
        copy_d[o].wait_recv()

    for h in range(2):
        lanes = pl.ds(h * LANE, LANE)
        for j in range(3):
            g1_ref[pl.ds(j * OUT_SH, OUT_SH), lanes] = outs[h, j]
        g1_ref[pl.ds(3 * OUT_SH, FEAT - 3 * OUT_SH), lanes] = outs[h, 3, 0:FEAT - 3 * OUT_SH, :]
        g2_ref[:, lanes] = outs[h, 3, FEAT_P - 3 * OUT_SH:FEAT_P - 3 * OUT_SH + CLS, :]
    loss_at = FEAT_P - 3 * OUT_SH + CLS
    loss_ref[...] = -outs[0, 3, loss_at:loss_at + 1, 0:1] / count

    for f in order:
        ex1[f - 1].wait_send()
        ex2[f - 1].wait_send()
        ex3[f - 1].wait_send()
        counts[f - 1].wait_send()
    for o in [0, 1, 2, 3]:
        copy_a[o].wait_send()
        copy_d[o].wait_send()
        if o:
            copy_b[o].wait_send()
            copy_c[o].wait_send()


def solution(mesh):
    vmem = pl.BlockSpec(memory_space=pltpu.VMEM)
    smem = pl.BlockSpec(memory_space=pltpu.SMEM)
    hbm = pl.BlockSpec(memory_space=pl.ANY)
    dma8 = pltpu.SemaphoreType.DMA((8,))
    dma4 = pltpu.SemaphoreType.DMA((4,))

    def device_step(feats, w_one, w_two, send_idx, send_count, edge_src, edge_wt, labels, label_mask):
        call = pl.pallas_call(
            kernel,
            out_shape=(jax.ShapeDtypeStruct((1, 1), F32), jax.ShapeDtypeStruct((FEAT, HID), F32),
                       jax.ShapeDtypeStruct((CLS, HID), F32)),
            in_specs=[hbm, hbm, hbm, vmem, smem, vmem, vmem, vmem, vmem],
            out_specs=(vmem, vmem, vmem),
            scratch_shapes=[
                pltpu.VMEM((FEAT, ROWS), BF16), pltpu.VMEM((FEAT_L, ROWS), BF16), pltpu.VMEM((FEAT, HID), F32),
                pltpu.VMEM((CLS, HID), F32), pltpu.VMEM((CLS_P, HID), BF16),
                pltpu.VMEM((HID, FEAT_P), BF16), pltpu.VMEM((DEG, ROWS), F32),
                pltpu.VMEM((EXT, ROWS), BF16), pltpu.VMEM((EXT, ROWS), BF16), pltpu.VMEM((EXT, ROWS), BF16),
                pltpu.VMEM((DEVS * HALO, ROWS), BF16), pltpu.VMEM((ROWS, DEVS * HALO), BF16),
                pltpu.VMEM((FEAT_P, ROWS), F32), pltpu.VMEM((FEAT_P, ROWS), BF16),
                pltpu.VMEM((HID, ROWS), BF16), pltpu.VMEM((ROWS, HID), BF16),
                pltpu.VMEM((DEVS * HALO, FEAT_L), BF16), pltpu.VMEM((DEVS * HALO, FEAT_L), BF16),
                pltpu.VMEM((DEVS * HALO, HID), BF16), pltpu.VMEM((DEVS * HALO, HID), BF16),
                pltpu.VMEM((DEVS * HALO, LANE), F32), pltpu.VMEM((DEVS * HALO, LANE), F32),
                pltpu.VMEM((8, LANE), F32), pltpu.VMEM((8, 8, LANE), F32),
                pltpu.VMEM((2, 4, OUT_SH, LANE), F32), pltpu.VMEM((4, OUT_SH, LANE), F32),
                pltpu.VMEM((4, OUT_SH, LANE), F32), pltpu.VMEM((4, OUT_SH, LANE), F32),
                pltpu.VMEM((2, 4, OUT_SH, LANE), F32),
                dma4, dma8, dma8, dma8, dma8, dma8, dma8, dma8, dma8,
                dma4, dma4, dma4, dma4, dma4, dma4, dma4, dma4,
            ],
            compiler_params=pltpu.CompilerParams(
                collective_id=0, has_side_effects=True, vmem_limit_bytes=56 * 1024 * 1024),
            name="gcn_step",
        )
        loss, grad_one, grad_two = call(
            feats.T, w_one, w_two.T, send_idx, send_count, edge_src.T, edge_wt.T,
            labels.reshape(1, ROWS), label_mask.reshape(1, ROWS))
        return loss.reshape(()), grad_one, grad_two.T

    row_spec = P("graph", None)
    vec_spec = P("graph")
    return jax.shard_map(
        device_step, mesh=mesh,
        in_specs=(row_spec, P(), P(), row_spec, vec_spec, row_spec, row_spec, vec_spec, vec_spec),
        out_specs=(P(), P(), P()), check_vma=False)
```

time: 390 us -> 62.4 us (0.16)
  local copies, waits for them, and re-layouts: 145 us -> 2.57 us
  other arithmetic: 131 us -> 0 us
  Pallas kernels: 0 us -> 57.2 us
  blocking collectives: 47.2 us -> 0 us
  waiting for transfers between devices: 35.3 us -> 0 us
  between operations: 16.8 us -> 2.36 us
  starting transfers between devices: 9.37 us -> 0 us
    gather x4 -> x0, local copies, waits for them, and re-layouts: 136 us -> none  [the longest x2 132 us: aggregate(): ext_rows[edge_src].astype(jnp.float32) * edge_wt[:, :, None]]
    scatter-add x2 -> x0, other arithmetic: 92.8 us -> none  [the longest x1 88.5 us: device_step(): jax.ops.segment_sum(contrib, flat_src, num_segments=row_count + dev_count...]
    pallas_call x0 -> x1, Pallas kernels: none -> 57.2 us  [device_step(): call(feats.T, w_one, w_two.T, send_idx, send_count, edge_src.T, edge_wt.T...]
    psum x2 -> x0, blocking collectives: 47.2 us -> none  [the longest x1 24 us: device_step(): label_total = lax.psum(jnp.sum(mask_f), 'graph')]
    reduce_sum x5 -> x0, other arithmetic: 25.7 us -> none  [the longest x2 24.4 us: aggregate(): jnp.sum(ext_rows[edge_src].astype(jnp.float32) * edge_wt[:, :, None], axi...]
    all_to_all x3 -> x0, waiting for transfers between devices: 18.9 us -> none  [the longest x2 9.69 us: aggregate(): incoming = lax.all_to_all(outgoing, 'graph', 0, 0, tiled=True)]
    psum x1 -> x0, waiting for transfers between devices: 16.3 us -> none  [device_step(): lax.psum(jnp.einsum('nf,nh->fh', z_one, d_y1, preferred_element_type=jnp....]
    all_to_all x3 -> x0, starting transfers between devices: 9.33 us -> none  [the longest x2 6.45 us: aggregate(): incoming = lax.all_to_all(outgoing, 'graph', 0, 0, tiled=True)]
  transfers between devices with their start and end apart: 4 -> 0, of which waited for: 3 -> 0; matrix products, arithmetic and copies ran while one was open for 1% -> 0% of each run, Pallas kernels for 0% -> 0%
where the time goes in v1:
time: 62.4 us; the launch traced here: 62.2 us
  Pallas kernels  57.2 us (92%)
  local copies, waits for them, and re-layouts  2.57 us (4%)
  between operations  2.36 us (4%)
    pallas_call x1, Pallas kernels, device_step(): call(feats.T, w_one, w_two.T, send_idx, send_count, edge_src.T, edge_wt.T...  57.2 us
    unnamed x4, local copies, waits for them, and re-layouts  2.57 us

profile of v1, /device:TPU:0, one launch (start us, length us, event | category | flops | bytes accessed | tf_op | source)
XLA Modules:
  0.0 62.2 jit_solution(5975594907559283073)
XLA Ops:
  0.6 57.2 %gcn_step.1 = (f32[1,1]{1,0:T(1,128)}, f32[602,256]{1,0:T(8,128)}, f32[41,256]{1,0:T(8,128)}) custom-call(bf16[602,1024]{1,0:T(8,128)(2,1)} %bitcast.8, f32[602,256]{1,0:T(8,128)} %w_one_h.1, f32[41,256]{1,0:T(8,128)} %bitcast.12, s32[8,64]{1,0:T(8,128)} %idx_ref.1, s32[8]{0:T(128)} %cnt_ref.1, s32[16,1024]{1,0:T(8,128)} %bitcast.9, f32[16,1024]{1,0:T(8,128)} %bitcast.10, ...), custom_call_target="tpu_custom_call" | custom-call | tf_op jit(solution)/shard_map/gcn_step/pallas_call | solution.py:356
  57.9 0.0 copy-start
  58.5 1.9 %copy.16 = f32[602,256]{1,0:T(8,128)} copy(f32[602,256]{1,0:T(8,128)} %get-tuple-element.13) | data formatting | bytes 1232896
  60.4 0.0 copy-done
  60.4 0.6 copy.17
Async XLA Ops:
  57.9 2.5 %copy-start = (f32[41,256]{1,0:T(8,128)S(1)}, f32[41,256]{1,0:T(8,128)}, u32[]{:S(2)}) copy-start(f32[41,256]{1,0:T(8,128)} %get-tuple-element.8) | copy-start | bytes 125956

commit v2 on v1

v2 whole, which is shorter than its diff:
```python
import jax
import jax.numpy as jnp
from jax import lax
from jax.experimental import pallas as pl
from jax.experimental.pallas import tpu as pltpu
from jax.sharding import PartitionSpec as P

MESH = pl.DeviceIdType.MESH
F32 = jnp.float32
BF16 = jnp.bfloat16

DEVS = 8
ROWS = 1024
HALO = 64
DEG = 16
EXT = ROWS + (DEVS - 1) * HALO
FEAT = 602
FEAT_P = 608
FEAT_L = 640
HID = 256
CLS = 41
CLS_P = 48
OUT_SH = 168
LANE = 128
TILE = 512
TILES = ROWS // TILE
HALOS = (DEVS - 1) * HALO
SLOTS = [6, 7, 4, 1, 2, 5, 3]
EARLY = 4
SUBS = 3
SUB = OUT_SH // SUBS


def dot_nn(a, b):
    return lax.dot_general(a, b, (((1,), (0,)), ((), ())), preferred_element_type=F32)


def dot_nt(a, b):
    return lax.dot_general(a, b, (((1,), (1,)), ((), ())), preferred_element_type=F32)


def split3(x):
    hi = x.astype(BF16)
    rest = x - hi.astype(F32)
    mid = rest.astype(BF16)
    low = (rest - mid.astype(F32)).astype(BF16)
    return hi, mid, low


def iota(shape, dim):
    return lax.broadcasted_iota(jnp.int32, shape, dim)


def kernel(feats_h, w_one_h, w_two_h, idx_h, cnt_h, src_h, wt_h, lab_h, mask_h,
           loss_ref, g1_ref, g2_ref,
           idx_ref, cnt_ref, src_ref, wt_ref, lab_ref, mask_ref,
           feats_raw, feats_t, w_one_f, w_two_f, w_two_p, w_one_t, wts, row_ids, at_0, at_1, sel, sel_t,
           z1_acc, z1_t, z2_acc, z2_s, h1_t, h1_n, x1, halo1, x2, halo2, th, tret, cnt_src, cnt_in,
           grads, a_in, b_out, b_in, outs,
           in_sem, s1, r1, sc, rc, s2, r2, s3, r3, sa, ra, sb, rb, so, ro, sd, rd):
    me = lax.axis_index("graph")
    core = me % 2
    chip = me // 2
    cx = chip % 2
    cy = chip // 2

    def flip_chip(f):
        fx, fy = f % 2, f // 2
        nx = 1 - cx if fx else cx
        ny = 1 - cy if fy else cy
        return ny * 2 + nx

    def flip_dev(f):
        nc = 1 - core if f % 2 else core
        return flip_chip(f // 2) * 2 + nc

    peers = [flip_dev(f) for f in SLOTS]

    barrier = pltpu.get_barrier_semaphore()
    for peer in peers:
        pl.semaphore_signal(barrier, inc=1, device_id=(peer,), device_id_type=MESH)

    pairs = [(idx_h, idx_ref), (cnt_h, cnt_ref), (feats_h, feats_raw), (src_h, src_ref), (wt_h, wt_ref),
             (mask_h, mask_ref), (lab_h, lab_ref), (w_one_h, w_one_f), (w_two_h, w_two_f)]
    loads = [pltpu.make_async_copy(a, b, in_sem.at[n]) for n, (a, b) in enumerate(pairs)]
    for load in loads:
        load.start()
    ats = [at_0, at_1]

    row_ids[pl.ds(0, ROWS), :] = iota((ROWS, LANE), 0)
    for p, peer in enumerate(peers):
        row_ids[pl.ds(ROWS + p * HALO, HALO), :] = iota((HALO, LANE), 0) + (ROWS + peer * HALO)

    loads[0].wait()
    loads[1].wait()
    eye = iota((HALO, HALO), 0) == iota((HALO, HALO), 1)
    for p, peer in enumerate(peers):
        row = jnp.where(iota((1, HALO), 1) < cnt_ref[peer], idx_ref[pl.ds(peer, 1), :], -1).astype(F32)
        col = jnp.sum(jnp.where(eye, jnp.broadcast_to(row, (HALO, HALO)), 0.0), axis=1, keepdims=True)
        col = col.astype(jnp.int32)
        hot = iota((HALO, ROWS), 1) == jnp.broadcast_to(col, (HALO, ROWS))
        sel[pl.ds(p * HALO, HALO), :] = jnp.where(hot, 1.0, 0.0).astype(BF16)

    loads[5].wait()
    mask_f = mask_ref[...].astype(F32)
    own_count = jnp.sum(mask_f, axis=1, keepdims=True)
    cnt_src[...] = jnp.broadcast_to(own_count, (8, LANE))

    loads[3].wait()
    loads[4].wait()
    src = src_ref[...]
    wt = wt_ref[...]
    krow = iota((DEG, ROWS), 0)
    total = wt
    for d in range(1, DEG):
        same = (pltpu.roll(src, d, 0) == src) & (krow >= d)
        total = total + jnp.where(same, pltpu.roll(wt, d, 0), 0.0)
    wts[...] = total

    def build(t, half, start, count, step=32):
        for lane in range(2):
            at_lane = (half * 2 + lane) * LANE
            lanes = pl.ds(t * TILE + at_lane, LANE)
            source = src_ref[:, lanes]
            weight = wts[:, lanes]
            sources = [jnp.broadcast_to(source[k:k + 1, :], (step, LANE)) for k in range(DEG)]
            weights = [jnp.broadcast_to(weight[k:k + 1, :], (step, LANE)) for k in range(DEG)]
            for part in range(count // step):
                here = pl.ds(pl.multiple_of(start + part * step, step), step)
                rows = row_ids[here, :]
                acc = jnp.zeros((step, LANE), F32)
                for k in range(DEG):
                    acc = jnp.where(rows == sources[k], weights[k], acc)
                for n, term in enumerate(split3(acc)):
                    ats[t][n, here, pl.ds(at_lane, LANE)] = term

    def build_all(t, first, count, size):
        for half in range(2):
            def stage(i, carry, half=half):
                build(t, half, pl.multiple_of(first + i * size, size), size)
                return carry

            if count == size:
                build(t, half, first, size)
            else:
                lax.fori_loop(0, count // size, stage, 0)

    def aggregate(left, first, count, t):
        rows = pl.ds(first, count)
        return (dot_nn(left, ats[t][0, rows, :]) + dot_nn(left, ats[t][1, rows, :])
                + dot_nn(left, ats[t][2, rows, :]))

    def cols_of(t):
        return pl.ds(t * TILE, TILE)

    loads[2].wait()
    feats_t[pl.ds(592, FEAT_L - 592), :] = jnp.zeros((FEAT_L - 592, ROWS), BF16)
    feats_t[pl.ds(0, FEAT), :] = feats_raw[...]

    def exchange(src, dst, send, recv):
        return [pltpu.make_async_remote_copy(
            src_ref=src.at[pl.ds(p * HALO, HALO), :], dst_ref=dst.at[pl.ds(p * HALO, HALO), :],
            send_sem=send.at[p], recv_sem=recv.at[p], device_id=(peer,), device_id_type=MESH)
            for p, peer in enumerate(peers)]

    early = pl.ds(0, EARLY * HALO)
    late = pl.ds(EARLY * HALO, HALOS - EARLY * HALO)
    ex1 = exchange(x1, halo1, s1, r1)
    x1[early, :] = dot_nt(sel[early, :], feats_t[...]).astype(BF16)
    pl.semaphore_wait(barrier, DEVS - 1)
    for p in range(EARLY):
        ex1[p].start()
    x1[late, :] = dot_nt(sel[late, :], feats_t[...]).astype(BF16)
    for p in range(EARLY, DEVS - 1):
        ex1[p].start()
    counts = []
    for p, peer in enumerate(peers):
        counts.append(pltpu.make_async_remote_copy(
            src_ref=cnt_src, dst_ref=cnt_in.at[p], send_sem=sc.at[p], recv_sem=rc.at[p],
            device_id=(peer,), device_id_type=MESH))
        counts[-1].start()

    for t in range(TILES):
        build_all(t, 0, ROWS, 256)
        z1_acc[:, cols_of(t)] = aggregate(feats_t[pl.ds(0, FEAT_P), :], 0, ROWS, t)

    for t in range(TILES):
        build_all(t, ROWS, HALOS, 448)

    sel_t[...] = sel[...].T

    loads[6].wait()
    loads[7].wait()
    loads[8].wait()
    w_one_t[:, pl.ds(512, FEAT_P - 512)] = jnp.zeros((HID, FEAT_P - 512), BF16)
    w_one_t[:, pl.ds(0, FEAT)] = w_one_f[...].T.astype(BF16)
    w_two_p[...] = jnp.zeros((CLS_P, HID), BF16)
    w_two_p[pl.ds(0, CLS), :] = w_two_f[...].astype(BF16)
    w_two_b = w_two_p[...]
    w_stack = jnp.concatenate(
        [jnp.concatenate([w_two_b.astype(F32), jnp.zeros((LANE - CLS_P, HID), F32)], axis=0)] * 3, axis=0).astype(BF16)

    for p in range(EARLY):
        ex1[p].wait_recv()
    halo1_t = halo1[early, :].T[:FEAT_P, :]
    for t in range(TILES):
        z1_acc[:, cols_of(t)] = z1_acc[:, cols_of(t)] + aggregate(halo1_t, ROWS, EARLY * HALO, t)
    for p in range(EARLY, DEVS - 1):
        ex1[p].wait_recv()
    halo1_t = halo1[late, :].T[:FEAT_P, :]
    for t in range(TILES):
        z1_t[:, cols_of(t)] = (z1_acc[:, cols_of(t)] + aggregate(
            halo1_t, ROWS + EARLY * HALO, HALOS - EARLY * HALO, t)).astype(BF16)

    h1_t[...] = jnp.maximum(dot_nn(w_one_t[...], z1_t[...]), 0.0).astype(BF16)
    x2[...] = dot_nt(sel[...], h1_t[...]).astype(BF16)
    ex2 = exchange(x2, halo2, s2, r2)
    for copy in ex2:
        copy.start()

    h1_n[...] = h1_t[...].T
    for t in range(TILES):
        z2_acc[:, cols_of(t)] = aggregate(h1_t[...], 0, ROWS, t)
    for copy in ex2:
        copy.wait_recv()
    halo2_t = halo2[...].T
    for t in range(TILES):
        z2_s[:, cols_of(t)] = (z2_acc[:, cols_of(t)] + aggregate(halo2_t, ROWS, HALOS, t)).astype(BF16)
    z2_t = z2_s[...]

    count = cnt_src[...]
    for p in range(DEVS - 1):
        counts[p].wait_recv()
        count = count + cnt_in[p]
    count = count[0:1, 0:1]

    logits = dot_nn(w_two_b, z2_t)
    cls_row = iota((CLS_P, ROWS), 0)
    real = cls_row < CLS
    top = jnp.max(jnp.where(real, logits, -3.0e38), axis=0, keepdims=True)
    shifted = logits - top
    expo = jnp.where(real, jnp.exp(shifted), 0.0)
    log_prob = shifted - jnp.log(jnp.sum(expo, axis=0, keepdims=True))
    hit = cls_row == lab_ref[...]
    loss_row = jnp.sum(jnp.where(hit, log_prob, 0.0), axis=0, keepdims=True) * mask_f
    scale = mask_f / count
    d_log = (jnp.exp(log_prob) - jnp.where(hit, 1.0, 0.0)) * scale
    g2_t = jnp.where(real, d_log, 0.0).astype(BF16)
    g2_n = jnp.concatenate([g2_t.astype(F32), jnp.zeros((LANE - CLS_P, ROWS), F32)], axis=0).T.astype(BF16)

    def scatter(first, rows_n):
        rows = pl.ds(first, rows_n)
        out = jnp.zeros((rows_n, LANE), F32)
        for t in range(TILES):
            for n in range(3):
                out = out + dot_nn(ats[t][n, rows, :], g2_n[t * TILE:(t + 1) * TILE, :])
        return out

    th[...] = scatter(ROWS, HALOS)
    ex3 = exchange(th, tret, s3, r3)
    for copy in ex3:
        copy.start()

    own_t = scatter(0, ROWS)
    grad_two = dot_nt(g2_t, z2_t)
    loss_sum = jnp.sum(loss_row, axis=1, keepdims=True)
    grad_two = jnp.where(iota((CLS_P, HID), 0) == CLS, jnp.broadcast_to(loss_sum, (CLS_P, HID)), grad_two)

    for copy in ex3:
        copy.wait_recv()
    back = dot_nn(sel_t[...], jnp.concatenate(split3(tret[...]), axis=1))
    own_t = own_t + (back[:, 0:LANE] + back[:, LANE:2 * LANE] + back[:, 2 * LANE:3 * LANE])
    d_h1 = dot_nn(jnp.concatenate(split3(own_t), axis=1), w_stack)
    g1_b = jnp.where(h1_n[...].astype(F32) > 0, d_h1, 0.0).astype(BF16)
    grad_one = dot_nn(z1_t[...], g1_b)

    for h in range(2):
        lanes = slice(h * LANE, (h + 1) * LANE)
        for j in range(3):
            grads[h, j] = grad_one[j * OUT_SH:(j + 1) * OUT_SH, lanes]
        grads[h, 3, pl.ds(0, FEAT_P - 3 * OUT_SH), :] = grad_one[3 * OUT_SH:FEAT_P, lanes]
        grads[h, 3, pl.ds(FEAT_P - 3 * OUT_SH, CLS_P), :] = grad_two[:, lanes]
        grads[h, 3, pl.ds(FEAT_P - 3 * OUT_SH + CLS_P, 16), :] = jnp.zeros((16, LANE), F32)

    mate = flip_dev(1)
    flips = [3, 1, 2]

    def part(u):
        return pl.ds(u * SUB, SUB)

    copy_a, copy_b, copy_c, copy_d = {}, {}, {}, {}
    for u in range(SUBS):
        for o in flips + [0]:
            to_chip = flip_chip(o)
            copy_a[o, u] = pltpu.make_async_remote_copy(
                src_ref=grads.at[1 - core, to_chip, part(u), :], dst_ref=a_in.at[o, part(u), :],
                send_sem=sa.at[o, u], recv_sem=ra.at[o, u], device_id=(mate,), device_id_type=MESH)
            copy_a[o, u].start()
    for u in range(SUBS):
        for o in flips:
            to_chip = flip_chip(o)
            copy_a[o, u].wait_recv()
            b_out[o, part(u), :] = grads[core, to_chip, part(u), :] + a_in[o, part(u), :]
            copy_b[o, u] = pltpu.make_async_remote_copy(
                src_ref=b_out.at[o, part(u), :], dst_ref=b_in.at[o, part(u), :],
                send_sem=sb.at[o, u], recv_sem=rb.at[o, u],
                device_id=(to_chip * 2 + core,), device_id_type=MESH)
            copy_b[o, u].start()

    def to_mate(o, u):
        at_chip = flip_chip(o)
        copy_d[o, u] = pltpu.make_async_remote_copy(
            src_ref=outs.at[core, at_chip, part(u), :], dst_ref=outs.at[core, at_chip, part(u), :],
            send_sem=sd.at[o, u], recv_sem=rd.at[o, u], device_id=(mate,), device_id_type=MESH)
        copy_d[o, u].start()

    for u in range(SUBS):
        copy_a[0, u].wait_recv()
        mine = grads[core, chip, part(u), :] + a_in[0, part(u), :]
        for o in flips:
            copy_b[o, u].wait_recv()
        outs[core, chip, part(u), :] = mine + (
            (b_in[1, part(u), :] + b_in[2, part(u), :]) + b_in[3, part(u), :])
        for o in flips:
            copy_c[o, u] = pltpu.make_async_remote_copy(
                src_ref=outs.at[core, chip, part(u), :], dst_ref=outs.at[core, chip, part(u), :],
                send_sem=so.at[o, u], recv_sem=ro.at[o, u],
                device_id=(flip_chip(o) * 2 + core,), device_id_type=MESH)
            copy_c[o, u].start()
        to_mate(0, u)
    for u in range(SUBS):
        for o in [1, 2, 3]:
            copy_c[o, u].wait_recv()
            to_mate(o, u)
    for u in range(SUBS):
        for o in [0, 1, 2, 3]:
            copy_d[o, u].wait_recv()

    for h in range(2):
        lanes = pl.ds(h * LANE, LANE)
        for j in range(3):
            g1_ref[pl.ds(j * OUT_SH, OUT_SH), lanes] = outs[h, j]
        g1_ref[pl.ds(3 * OUT_SH, FEAT - 3 * OUT_SH), lanes] = outs[h, 3, 0:FEAT - 3 * OUT_SH, :]
        g2_ref[:, lanes] = outs[h, 3, FEAT_P - 3 * OUT_SH:FEAT_P - 3 * OUT_SH + CLS, :]
    loss_at = FEAT_P - 3 * OUT_SH + CLS
    loss_ref[...] = -outs[0, 3, loss_at:loss_at + 1, 0:1] / count

    for copy in ex1 + ex2 + ex3 + counts:
        copy.wait_send()
    for group in (copy_a, copy_b, copy_c, copy_d):
        for copy in group.values():
            copy.wait_send()


def solution(mesh):
    vmem = pl.BlockSpec(memory_space=pltpu.VMEM)
    hbm = pl.BlockSpec(memory_space=pl.ANY)
    dma8 = pltpu.SemaphoreType.DMA((8,))
    dma_sum = pltpu.SemaphoreType.DMA((4, SUBS))

    def device_step(feats, w_one, w_two, send_idx, send_count, edge_src, edge_wt, labels, label_mask):
        call = pl.pallas_call(
            kernel,
            out_shape=(pltpu.VMEM((1, 1), F32), pltpu.VMEM((FEAT, HID), F32),
                       pltpu.VMEM((CLS, HID), F32)),
            in_specs=[hbm] * 9,
            out_specs=(vmem, vmem, vmem),
            scratch_shapes=[
                pltpu.VMEM((DEVS, HALO), jnp.int32), pltpu.SMEM((DEVS,), jnp.int32),
                pltpu.VMEM((DEG, ROWS), jnp.int32), pltpu.VMEM((DEG, ROWS), F32),
                pltpu.VMEM((1, ROWS), jnp.int32), pltpu.VMEM((1, ROWS), jnp.int32),
                pltpu.VMEM((FEAT, ROWS), BF16), pltpu.VMEM((FEAT_L, ROWS), BF16), pltpu.VMEM((FEAT, HID), F32),
                pltpu.VMEM((CLS, HID), F32), pltpu.VMEM((CLS_P, HID), BF16),
                pltpu.VMEM((HID, FEAT_P), BF16), pltpu.VMEM((DEG, ROWS), F32), pltpu.VMEM((EXT, LANE), jnp.int32),
                pltpu.VMEM((3, EXT, TILE), BF16), pltpu.VMEM((3, EXT, TILE), BF16),
                pltpu.VMEM((HALOS, ROWS), BF16), pltpu.VMEM((ROWS, HALOS), BF16),
                pltpu.VMEM((FEAT_P, ROWS), F32), pltpu.VMEM((FEAT_P, ROWS), BF16),
                pltpu.VMEM((HID, ROWS), F32), pltpu.VMEM((HID, ROWS), BF16),
                pltpu.VMEM((HID, ROWS), BF16), pltpu.VMEM((ROWS, HID), BF16),
                pltpu.VMEM((HALOS, FEAT_L), BF16), pltpu.VMEM((HALOS, FEAT_L), BF16),
                pltpu.VMEM((HALOS, HID), BF16), pltpu.VMEM((HALOS, HID), BF16),
                pltpu.VMEM((HALOS, LANE), F32), pltpu.VMEM((HALOS, LANE), F32),
                pltpu.VMEM((8, LANE), F32), pltpu.VMEM((8, 8, LANE), F32),
                pltpu.VMEM((2, 4, OUT_SH, LANE), F32), pltpu.VMEM((4, OUT_SH, LANE), F32),
                pltpu.VMEM((4, OUT_SH, LANE), F32), pltpu.VMEM((4, OUT_SH, LANE), F32),
                pltpu.VMEM((2, 4, OUT_SH, LANE), F32),
                pltpu.SemaphoreType.DMA((9,)), dma8, dma8, dma8, dma8, dma8, dma8, dma8, dma8,
                dma_sum, dma_sum, dma_sum, dma_sum, dma_sum, dma_sum, dma_sum, dma_sum,
            ],
            compiler_params=pltpu.CompilerParams(
                collective_id=0, has_side_effects=True, vmem_limit_bytes=56 * 1024 * 1024),
            name="gcn_step",
        )
        loss, grad_one, grad_two = call(
            feats.T, w_one, w_two.T, send_idx, send_count, edge_src.T, edge_wt.T,
            labels.reshape(1, ROWS), label_mask.reshape(1, ROWS))
        return loss.reshape(()), grad_one, grad_two.T

    row_spec = P("graph", None)
    vec_spec = P("graph")
    return jax.shard_map(
        device_step, mesh=mesh,
        in_specs=(row_spec, P(), P(), row_spec, vec_spec, row_spec, row_spec, vec_spec, vec_spec),
        out_specs=(P(), P(), P()), check_vma=False)
```

time: 62.4 us -> 51.4 us (0.82)
  Pallas kernels: 57.2 us -> 48.1 us
  local copies, waits for them, and re-layouts: 2.57 us -> 1.45 us
    pallas_call x1, Pallas kernels: 57.2 us -> 48.1 us  [device_step(): call(feats.T, w_one, w_two.T, send_idx, send_count, edge_src.T, edge_wt.T...]
    unnamed x4 -> x2, local copies, waits for them, and re-layouts: 2.57 us -> 1.45 us
where the time goes in v2:
time: 51.4 us; the launch traced here: 51.3 us
  Pallas kernels  48.1 us (94%)
  between operations  1.81 us (4%)
  local copies, waits for them, and re-layouts  1.45 us (3%)
    pallas_call x1, Pallas kernels, device_step(): call(feats.T, w_one, w_two.T, send_idx, send_count, edge_src.T, edge_wt.T...  48.1 us
    unnamed x2, local copies, waits for them, and re-layouts  1.45 us

profile of v2, /device:TPU:0, one launch (start us, length us, event | category | flops | bytes accessed | tf_op | source)
XLA Modules:
  0.0 51.3 jit_solution(6577952277628458377)
XLA Ops:
  0.6 48.1 %gcn_step.1 = (f32[1,1]{1,0:T(1,128)S(1)}, f32[602,256]{1,0:T(8,128)S(1)}, f32[41,256]{1,0:T(8,128)S(1)}) custom-call(bf16[602,1024]{1,0:T(8,128)(2,1)} %bitcast.9, f32[602,256]{1,0:T(8,128)} %w_one_h.1, f32[41,256]{1,0:T(8,128)} %bitcast.12, s32[8,64]{1,0:T(8,128)} %idx_h.1, s32[8]{0:T(128)} %cnt_h.1, s32[16,1024]{1,0:T(8,128)} %bitcast.10, ...), custom_call_target="tpu_custom_call" | custom-call | tf_op jit(solution)/shard_map/gcn_step/pallas_call | solution.py:394
  48.7 0.8 %copy.16 = f32[602,256]{1,0:T(8,128)} copy(f32[602,256]{1,0:T(8,128)S(1)} %get-tuple-element.10) | data formatting | bytes 1232896
  49.6 0.6 %copy.17 = f32[256,41]{0,1:T(8,128)} copy(f32[256,41]{0,1:T(8,128)S(1)} %bitcast.8) | data formatting | bytes 83968

commit v3 on v2

--- a/solution.py
+++ b/solution.py
@@ -25,7 +25,7 @@
 TILE = 512
 TILES = ROWS // TILE
 HALOS = (DEVS - 1) * HALO
-SLOTS = [6, 7, 4, 1, 2, 5, 3]
+SLOTS = [6, 7, 4, 5, 2, 3, 1]
 EARLY = 4
 SUBS = 3
 SUB = OUT_SH // SUBS
@@ -54,8 +54,8 @@
 def kernel(feats_h, w_one_h, w_two_h, idx_h, cnt_h, src_h, wt_h, lab_h, mask_h,
            loss_ref, g1_ref, g2_ref,
            idx_ref, cnt_ref, src_ref, wt_ref, lab_ref, mask_ref,
-           feats_raw, feats_t, w_one_f, w_two_f, w_two_p, w_one_t, wts, row_ids, at_0, at_1, sel, sel_t,
-           z1_acc, z1_t, z2_acc, z2_s, h1_t, h1_n, x1, halo1, x2, halo2, th, tret, cnt_src, cnt_in,
+           feats_raw, feats_t, w_one_f, w_two_f, w_two_p, w_two_3, w_one_t, wts, row_ids, at_0, at_1, sel,
+           z1_acc, z1_t, z2_acc, z2_s, h1_t, x1, halo1, x2, halo2, th, tret, cnt_src, cnt_in,
            grads, a_in, b_out, b_in, outs,
            in_sem, s1, r1, sc, rc, s2, r2, s3, r3, sa, ra, sb, rb, so, ro, sd, rd):
     me = lax.axis_index("graph")
@@ -87,9 +87,19 @@
         load.start()
     ats = [at_0, at_1]
 
-    row_ids[pl.ds(0, ROWS), :] = iota((ROWS, LANE), 0)
+    def number_rows(i, carry):
+        start = pl.multiple_of(i * 32, 32)
+        row_ids[pl.ds(start, 32), :] = iota((32, LANE), 0) + start
+        return carry
+
+    lax.fori_loop(0, ROWS // 32, number_rows, 0)
     for p, peer in enumerate(peers):
-        row_ids[pl.ds(ROWS + p * HALO, HALO), :] = iota((HALO, LANE), 0) + (ROWS + peer * HALO)
+        def number_halo(i, carry, p=p, peer=peer):
+            start = pl.multiple_of(i * 32, 32)
+            row_ids[pl.ds(ROWS + p * HALO + start, 32), :] = iota((32, LANE), 0) + (ROWS + peer * HALO + start)
+            return carry
+
+        lax.fori_loop(0, HALO // 32, number_halo, 0)
 
     loads[0].wait()
     loads[1].wait()
@@ -117,33 +127,34 @@
         total = total + jnp.where(same, pltpu.roll(wt, d, 0), 0.0)
     wts[...] = total
 
-    def build(t, half, start, count, step=32):
-        for lane in range(2):
-            at_lane = (half * 2 + lane) * LANE
-            lanes = pl.ds(t * TILE + at_lane, LANE)
-            source = src_ref[:, lanes]
-            weight = wts[:, lanes]
-            sources = [jnp.broadcast_to(source[k:k + 1, :], (step, LANE)) for k in range(DEG)]
-            weights = [jnp.broadcast_to(weight[k:k + 1, :], (step, LANE)) for k in range(DEG)]
-            for part in range(count // step):
-                here = pl.ds(pl.multiple_of(start + part * step, step), step)
-                rows = row_ids[here, :]
-                acc = jnp.zeros((step, LANE), F32)
-                for k in range(DEG):
-                    acc = jnp.where(rows == sources[k], weights[k], acc)
-                for n, term in enumerate(split3(acc)):
-                    ats[t][n, here, pl.ds(at_lane, LANE)] = term
-
-    def build_all(t, first, count, size):
-        for half in range(2):
-            def stage(i, carry, half=half):
-                build(t, half, pl.multiple_of(first + i * size, size), size)
-                return carry
-
-            if count == size:
-                build(t, half, first, size)
-            else:
-                lax.fori_loop(0, count // size, stage, 0)
+    def build(t, lane, start, count, step=32):
+        lanes = pl.ds(pl.multiple_of(t * TILE + lane * LANE, LANE), LANE)
+        source = src_ref[:, lanes]
+        weight = wts[:, lanes]
+        sources = [jnp.broadcast_to(source[k:k + 1, :], (step, LANE)) for k in range(DEG)]
+        weights = [jnp.broadcast_to(weight[k:k + 1, :], (step, LANE)) for k in range(DEG)]
+        for piece in range(count // step):
+            here = pl.ds(pl.multiple_of(start + piece * step, step), step)
+            rows = row_ids[here, :]
+            acc = jnp.zeros((step, LANE), F32)
+            for k in range(DEG):
+                acc = jnp.where(rows == sources[k], weights[k], acc)
+            for n, term in enumerate(split3(acc)):
+                ats[t][n, here, pl.ds(pl.multiple_of(lane * LANE, LANE), LANE)] = term
+
+    def build_local(t):
+        def stage(i, carry):
+            build(t, i // 2, pl.multiple_of((i % 2) * 512, 512), 512)
+            return carry
+
+        lax.fori_loop(0, 8, stage, 0)
+
+    def build_halo(t):
+        def stage(i, carry):
+            build(t, i, ROWS, HALOS)
+            return carry
+
+        lax.fori_loop(0, 4, stage, 0)
 
     def aggregate(left, first, count, t):
         rows = pl.ds(first, count)
@@ -181,13 +192,11 @@
         counts[-1].start()
 
     for t in range(TILES):
-        build_all(t, 0, ROWS, 256)
+        build_local(t)
         z1_acc[:, cols_of(t)] = aggregate(feats_t[pl.ds(0, FEAT_P), :], 0, ROWS, t)
 
     for t in range(TILES):
-        build_all(t, ROWS, HALOS, 448)
-
-    sel_t[...] = sel[...].T
+        build_halo(t)
 
     loads[6].wait()
     loads[7].wait()
@@ -197,8 +206,6 @@
     w_two_p[...] = jnp.zeros((CLS_P, HID), BF16)
     w_two_p[pl.ds(0, CLS), :] = w_two_f[...].astype(BF16)
     w_two_b = w_two_p[...]
-    w_stack = jnp.concatenate(
-        [jnp.concatenate([w_two_b.astype(F32), jnp.zeros((LANE - CLS_P, HID), F32)], axis=0)] * 3, axis=0).astype(BF16)
 
     for p in range(EARLY):
         ex1[p].wait_recv()
@@ -213,12 +220,13 @@
             halo1_t, ROWS + EARLY * HALO, HALOS - EARLY * HALO, t)).astype(BF16)
 
     h1_t[...] = jnp.maximum(dot_nn(w_one_t[...], z1_t[...]), 0.0).astype(BF16)
-    x2[...] = dot_nt(sel[...], h1_t[...]).astype(BF16)
+    for part_rows in (pl.ds(0, HALOS // 2), pl.ds(HALOS // 2, HALOS // 2)):
+        x2[part_rows, :] = dot_nt(sel[part_rows, :], h1_t[...]).astype(BF16)
     ex2 = exchange(x2, halo2, s2, r2)
     for copy in ex2:
         copy.start()
 
-    h1_n[...] = h1_t[...].T
+    w_two_3[...] = jnp.concatenate([w_two_b.astype(F32)] * 3, axis=0).T.astype(BF16)
     for t in range(TILES):
         z2_acc[:, cols_of(t)] = aggregate(h1_t[...], 0, ROWS, t)
     for copy in ex2:
@@ -246,18 +254,21 @@
     scale = mask_f / count
     d_log = (jnp.exp(log_prob) - jnp.where(hit, 1.0, 0.0)) * scale
     g2_t = jnp.where(real, d_log, 0.0).astype(BF16)
-    g2_n = jnp.concatenate([g2_t.astype(F32), jnp.zeros((LANE - CLS_P, ROWS), F32)], axis=0).T.astype(BF16)
 
     def scatter(first, rows_n):
         rows = pl.ds(first, rows_n)
-        out = jnp.zeros((rows_n, LANE), F32)
+        out = jnp.zeros((CLS_P, rows_n), F32)
         for t in range(TILES):
             for n in range(3):
-                out = out + dot_nn(ats[t][n, rows, :], g2_n[t * TILE:(t + 1) * TILE, :])
+                out = out + dot_nt(g2_t[:, t * TILE:(t + 1) * TILE], ats[t][n, rows, :])
         return out
 
-    th[...] = scatter(ROWS, HALOS)
-    ex3 = exchange(th, tret, s3, r3)
+    th[:, pl.ds(0, HALOS)] = scatter(ROWS, HALOS)
+    th[:, pl.ds(HALOS, HALO)] = jnp.zeros((CLS_P, HALO), F32)
+    ex3 = [pltpu.make_async_remote_copy(
+        src_ref=th.at[:, pl.ds(p // 2 * LANE, LANE)], dst_ref=tret.at[p],
+        send_sem=s3.at[p], recv_sem=r3.at[p], device_id=(peer,), device_id_type=MESH)
+        for p, peer in enumerate(peers)]
     for copy in ex3:
         copy.start()
 
@@ -268,11 +279,16 @@
 
     for copy in ex3:
         copy.wait_recv()
-    back = dot_nn(sel_t[...], jnp.concatenate(split3(tret[...]), axis=1))
-    own_t = own_t + (back[:, 0:LANE] + back[:, LANE:2 * LANE] + back[:, 2 * LANE:3 * LANE])
-    d_h1 = dot_nn(jnp.concatenate(split3(own_t), axis=1), w_stack)
-    g1_b = jnp.where(h1_n[...].astype(F32) > 0, d_h1, 0.0).astype(BF16)
-    grad_one = dot_nn(z1_t[...], g1_b)
+    first_half = iota((CLS_P, LANE), 1) < HALO
+    blocks = [jnp.where(first_half, tret[2 * n], tret[2 * n + 1] if n < 3 else 0.0) for n in range(4)]
+    back_t = jnp.concatenate(blocks, axis=1)[:, :HALOS]
+    back = dot_nn(jnp.concatenate(split3(back_t), axis=0), sel[...])
+    own_t = own_t + (back[0:CLS_P] + back[CLS_P:2 * CLS_P] + back[2 * CLS_P:3 * CLS_P])
+    d_h1 = dot_nn(w_two_3[...], jnp.concatenate(split3(own_t), axis=0))
+    g1_b = jnp.where(h1_t[...].astype(F32) > 0, d_h1, 0.0).astype(BF16)
+    half_m = FEAT_P // 2
+    grad_one = jnp.concatenate([dot_nt(z1_t[pl.ds(0, half_m), :], g1_b),
+                                dot_nt(z1_t[pl.ds(half_m, half_m), :], g1_b)], axis=0)
 
     for h in range(2):
         lanes = slice(h * LANE, (h + 1) * LANE)
@@ -370,16 +386,16 @@
                 pltpu.VMEM((DEG, ROWS), jnp.int32), pltpu.VMEM((DEG, ROWS), F32),
                 pltpu.VMEM((1, ROWS), jnp.int32), pltpu.VMEM((1, ROWS), jnp.int32),
                 pltpu.VMEM((FEAT, ROWS), BF16), pltpu.VMEM((FEAT_L, ROWS), BF16), pltpu.VMEM((FEAT, HID), F32),
-                pltpu.VMEM((CLS, HID), F32), pltpu.VMEM((CLS_P, HID), BF16),
+                pltpu.VMEM((CLS, HID), F32), pltpu.VMEM((CLS_P, HID), BF16), pltpu.VMEM((HID, 3 * CLS_P), BF16),
                 pltpu.VMEM((HID, FEAT_P), BF16), pltpu.VMEM((DEG, ROWS), F32), pltpu.VMEM((EXT, LANE), jnp.int32),
                 pltpu.VMEM((3, EXT, TILE), BF16), pltpu.VMEM((3, EXT, TILE), BF16),
-                pltpu.VMEM((HALOS, ROWS), BF16), pltpu.VMEM((ROWS, HALOS), BF16),
+                pltpu.VMEM((HALOS, ROWS), BF16),
                 pltpu.VMEM((FEAT_P, ROWS), F32), pltpu.VMEM((FEAT_P, ROWS), BF16),
                 pltpu.VMEM((HID, ROWS), F32), pltpu.VMEM((HID, ROWS), BF16),
-                pltpu.VMEM((HID, ROWS), BF16), pltpu.VMEM((ROWS, HID), BF16),
+                pltpu.VMEM((HID, ROWS), BF16),
                 pltpu.VMEM((HALOS, FEAT_L), BF16), pltpu.VMEM((HALOS, FEAT_L), BF16),
                 pltpu.VMEM((HALOS, HID), BF16), pltpu.VMEM((HALOS, HID), BF16),
-                pltpu.VMEM((HALOS, LANE), F32), pltpu.VMEM((HALOS, LANE), F32),
+                pltpu.VMEM((CLS_P, 512), F32), pltpu.VMEM((7, CLS_P, LANE), F32),
                 pltpu.VMEM((8, LANE), F32), pltpu.VMEM((8, 8, LANE), F32),
                 pltpu.VMEM((2, 4, OUT_SH, LANE), F32), pltpu.VMEM((4, OUT_SH, LANE), F32),
                 pltpu.VMEM((4, OUT_SH, LANE), F32), pltpu.VMEM((4, OUT_SH, LANE), F32),

time: 51.4 us -> 49.4 us (0.961)
  Pallas kernels: 48.1 us -> 46 us
    pallas_call x1, Pallas kernels: 48.1 us -> 46 us  [device_step(): call(feats.T, w_one, w_two.T, send_idx, send_count, edge_src.T, edge_wt.T...]
where the time goes in v3:
time: 49.4 us; the launch traced here: 49.3 us
  Pallas kernels  46 us (93%)
  between operations  1.8 us (4%)
  local copies, waits for them, and re-layouts  1.45 us (3%)
    pallas_call x1, Pallas kernels, device_step(): call(feats.T, w_one, w_two.T, send_idx, send_count, edge_src.T, edge_wt.T...  46 us
    unnamed x2, local copies, waits for them, and re-layouts  1.45 us

profile of v3, /device:TPU:0, one launch (start us, length us, event | category | flops | bytes accessed | tf_op | source)
XLA Modules:
  0.0 49.3 jit_solution(1448113695836970419)
XLA Ops:
  0.6 46.0 %gcn_step.1 = (f32[1,1]{1,0:T(1,128)S(1)}, f32[602,256]{1,0:T(8,128)S(1)}, f32[41,256]{1,0:T(8,128)S(1)}) custom-call(bf16[602,1024]{1,0:T(8,128)(2,1)} %bitcast.9, f32[602,256]{1,0:T(8,128)} %w_one_h.1, f32[41,256]{1,0:T(8,128)} %bitcast.12, s32[8,64]{1,0:T(8,128)} %idx_h.1, s32[8]{0:T(128)} %cnt_h.1, s32[16,1024]{1,0:T(8,128)} %bitcast.10, ...), custom_call_target="tpu_custom_call" | custom-call | tf_op jit(solution)/shard_map/gcn_step/pallas_call | solution.py:410
  46.7 0.8 %copy.16 = f32[602,256]{1,0:T(8,128)} copy(f32[602,256]{1,0:T(8,128)S(1)} %get-tuple-element.10) | data formatting | bytes 1232896
  47.5 0.6 %copy.17 = f32[256,41]{0,1:T(8,128)} copy(f32[256,41]{0,1:T(8,128)S(1)} %bitcast.8) | data formatting | bytes 83968

commit v4 on v3

--- a/solution.py
+++ b/solution.py
@@ -28,6 +28,7 @@
 SLOTS = [6, 7, 4, 5, 2, 3, 1]
 EARLY = 4
 SUBS = 3
+AHEAD = 2
 SUB = OUT_SH // SUBS
 
 
@@ -52,11 +53,11 @@
 
 
 def kernel(feats_h, w_one_h, w_two_h, idx_h, cnt_h, src_h, wt_h, lab_h, mask_h,
-           loss_ref, g1_ref, g2_ref,
+           outs, count_ref,
            idx_ref, cnt_ref, src_ref, wt_ref, lab_ref, mask_ref,
            feats_raw, feats_t, w_one_f, w_two_f, w_two_p, w_two_3, w_one_t, wts, row_ids, at_0, at_1, sel,
            z1_acc, z1_t, z2_acc, z2_s, h1_t, x1, halo1, x2, halo2, th, tret, cnt_src, cnt_in,
-           grads, a_in, b_out, b_in, outs,
+           grads, a_in, b_out, b_in,
            in_sem, s1, r1, sc, rc, s2, r2, s3, r3, sa, ra, sb, rb, so, ro, sd, rd):
     me = lax.axis_index("graph")
     core = me % 2
@@ -142,12 +143,12 @@
             for n, term in enumerate(split3(acc)):
                 ats[t][n, here, pl.ds(pl.multiple_of(lane * LANE, LANE), LANE)] = term
 
-    def build_local(t):
+    def build_local(t, begin, end):
         def stage(i, carry):
             build(t, i // 2, pl.multiple_of((i % 2) * 512, 512), 512)
             return carry
 
-        lax.fori_loop(0, 8, stage, 0)
+        lax.fori_loop(begin, end, stage, 0)
 
     def build_halo(t):
         def stage(i, carry):
@@ -163,6 +164,8 @@
 
     def cols_of(t):
         return pl.ds(t * TILE, TILE)
+
+    build_local(0, 0, AHEAD)
 
     loads[2].wait()
     feats_t[pl.ds(592, FEAT_L - 592), :] = jnp.zeros((FEAT_L - 592, ROWS), BF16)
@@ -182,6 +185,9 @@
     for p in range(EARLY):
         ex1[p].start()
     x1[late, :] = dot_nt(sel[late, :], feats_t[...]).astype(BF16)
+    loads[7].wait()
+    w_one_t[:, pl.ds(512, FEAT_P - 512)] = jnp.zeros((HID, FEAT_P - 512), BF16)
+    w_one_t[:, pl.ds(0, FEAT)] = w_one_f[...].T.astype(BF16)
     for p in range(EARLY, DEVS - 1):
         ex1[p].start()
     counts = []
@@ -192,20 +198,11 @@
         counts[-1].start()
 
     for t in range(TILES):
-        build_local(t)
+        build_local(t, 0 if t else AHEAD, 8)
         z1_acc[:, cols_of(t)] = aggregate(feats_t[pl.ds(0, FEAT_P), :], 0, ROWS, t)
 
     for t in range(TILES):
         build_halo(t)
-
-    loads[6].wait()
-    loads[7].wait()
-    loads[8].wait()
-    w_one_t[:, pl.ds(512, FEAT_P - 512)] = jnp.zeros((HID, FEAT_P - 512), BF16)
-    w_one_t[:, pl.ds(0, FEAT)] = w_one_f[...].T.astype(BF16)
-    w_two_p[...] = jnp.zeros((CLS_P, HID), BF16)
-    w_two_p[pl.ds(0, CLS), :] = w_two_f[...].astype(BF16)
-    w_two_b = w_two_p[...]
 
     for p in range(EARLY):
         ex1[p].wait_recv()
@@ -220,12 +217,19 @@
             halo1_t, ROWS + EARLY * HALO, HALOS - EARLY * HALO, t)).astype(BF16)
 
     h1_t[...] = jnp.maximum(dot_nn(w_one_t[...], z1_t[...]), 0.0).astype(BF16)
-    for part_rows in (pl.ds(0, HALOS // 2), pl.ds(HALOS // 2, HALOS // 2)):
-        x2[part_rows, :] = dot_nt(sel[part_rows, :], h1_t[...]).astype(BF16)
     ex2 = exchange(x2, halo2, s2, r2)
-    for copy in ex2:
+    x2[early, :] = dot_nt(sel[early, :], h1_t[...]).astype(BF16)
+    for copy in ex2[:EARLY]:
         copy.start()
-
+    x2[late, :] = dot_nt(sel[late, :], h1_t[...]).astype(BF16)
+    for copy in ex2[EARLY:]:
+        copy.start()
+
+    loads[6].wait()
+    loads[8].wait()
+    w_two_p[...] = jnp.zeros((CLS_P, HID), BF16)
+    w_two_p[pl.ds(0, CLS), :] = w_two_f[...].astype(BF16)
+    w_two_b = w_two_p[...]
     w_two_3[...] = jnp.concatenate([w_two_b.astype(F32)] * 3, axis=0).T.astype(BF16)
     for t in range(TILES):
         z2_acc[:, cols_of(t)] = aggregate(h1_t[...], 0, ROWS, t)
@@ -352,6 +356,16 @@
         for o in [0, 1, 2, 3]:
             copy_d[o, u].wait_recv()
 
+    count_ref[...] = jnp.broadcast_to(count, (8, LANE))
+
+    for copy in ex1 + ex2 + ex3 + counts:
+        copy.wait_send()
+    for group in (copy_a, copy_b, copy_c, copy_d):
+        for copy in group.values():
+            copy.wait_send()
+
+
+def lay_out(outs, count_ref, loss_ref, g1_ref, g2_ref):
     for h in range(2):
         lanes = pl.ds(h * LANE, LANE)
         for j in range(3):
@@ -359,13 +373,7 @@
         g1_ref[pl.ds(3 * OUT_SH, FEAT - 3 * OUT_SH), lanes] = outs[h, 3, 0:FEAT - 3 * OUT_SH, :]
         g2_ref[:, lanes] = outs[h, 3, FEAT_P - 3 * OUT_SH:FEAT_P - 3 * OUT_SH + CLS, :]
     loss_at = FEAT_P - 3 * OUT_SH + CLS
-    loss_ref[...] = -outs[0, 3, loss_at:loss_at + 1, 0:1] / count
-
-    for copy in ex1 + ex2 + ex3 + counts:
-        copy.wait_send()
-    for group in (copy_a, copy_b, copy_c, copy_d):
-        for copy in group.values():
-            copy.wait_send()
+    loss_ref[...] = -outs[0, 3, loss_at:loss_at + 1, 0:1] / count_ref[0:1, 0:1]
 
 
 def solution(mesh):
@@ -377,10 +385,9 @@
     def device_step(feats, w_one, w_two, send_idx, send_count, edge_src, edge_wt, labels, label_mask):
         call = pl.pallas_call(
             kernel,
-            out_shape=(pltpu.VMEM((1, 1), F32), pltpu.VMEM((FEAT, HID), F32),
-                       pltpu.VMEM((CLS, HID), F32)),
+            out_shape=(pltpu.VMEM((2, 4, OUT_SH, LANE), F32), pltpu.VMEM((8, LANE), F32)),
             in_specs=[hbm] * 9,
-            out_specs=(vmem, vmem, vmem),
+            out_specs=(vmem, vmem),
             scratch_shapes=[
                 pltpu.VMEM((DEVS, HALO), jnp.int32), pltpu.SMEM((DEVS,), jnp.int32),
                 pltpu.VMEM((DEG, ROWS), jnp.int32), pltpu.VMEM((DEG, ROWS), F32),
@@ -399,7 +406,6 @@
                 pltpu.VMEM((8, LANE), F32), pltpu.VMEM((8, 8, LANE), F32),
                 pltpu.VMEM((2, 4, OUT_SH, LANE), F32), pltpu.VMEM((4, OUT_SH, LANE), F32),
                 pltpu.VMEM((4, OUT_SH, LANE), F32), pltpu.VMEM((4, OUT_SH, LANE), F32),
-                pltpu.VMEM((2, 4, OUT_SH, LANE), F32),
                 pltpu.SemaphoreType.DMA((9,)), dma8, dma8, dma8, dma8, dma8, dma8, dma8, dma8,
                 dma_sum, dma_sum, dma_sum, dma_sum, dma_sum, dma_sum, dma_sum, dma_sum,
             ],
@@ -407,9 +413,15 @@
                 collective_id=0, has_side_effects=True, vmem_limit_bytes=56 * 1024 * 1024),
             name="gcn_step",
         )
-        loss, grad_one, grad_two = call(
+        outs, count = call(
             feats.T, w_one, w_two.T, send_idx, send_count, edge_src.T, edge_wt.T,
             labels.reshape(1, ROWS), label_mask.reshape(1, ROWS))
+        loss, grad_one, grad_two = pl.pallas_call(
+            lay_out,
+            out_shape=(jax.ShapeDtypeStruct((1, 1), F32), jax.ShapeDtypeStruct((FEAT, HID), F32),
+                       jax.ShapeDtypeStruct((CLS, HID), F32)),
+            in_specs=[vmem, vmem], out_specs=(vmem, vmem, vmem), name="gcn_results",
+        )(*(pltpu.with_memory_space_constraint(x, pltpu.VMEM) for x in (outs, count)))
         return loss.reshape(()), grad_one, grad_two.T
 
     row_spec = P("graph", None)

time: 49.4 us -> 47.6 us (0.964)
  local copies, waits for them, and re-layouts: 1.45 us -> 0 us
  between operations: 1.8 us -> 0.64 us
  Pallas kernels: 46 us -> 46.9 us
    unnamed x2 -> x0, local copies, waits for them, and re-layouts: 1.45 us -> none
    pallas_call x0 -> x1, Pallas kernels: none -> 0.88 us  [device_step(): pl.pallas_call(lay_out, out_shape=(jax.ShapeDtypeStruct((1, 1), F32), jax...]
where the time goes in v4:
time: 47.6 us; the launch traced here: 47.5 us
  Pallas kernels  46.9 us (99%)
  between operations  0.64 us (1%)
    pallas_call x1, Pallas kernels, device_step(): call(feats.T, w_one, w_two.T, send_idx, send_count, edge_src.T, edge_wt.T...  46 us

profile of v4, /device:TPU:0, one launch (start us, length us, event | category | flops | bytes accessed | tf_op | source)
XLA Modules:
  0.0 47.5 jit_solution(9489527548011256520)
XLA Ops:
  0.6 46.0 %gcn_step.1 = (f32[2,4,168,128]{3,2,1,0:T(8,128)S(1)}, f32[8,128]{1,0:T(8,128)S(1)}) custom-call(bf16[602,1024]{1,0:T(8,128)(2,1)} %bitcast.8, f32[602,256]{1,0:T(8,128)} %w_one_h.1, f32[41,256]{1,0:T(8,128)} %bitcast.11, s32[8,64]{1,0:T(8,128)} %idx_h.1, s32[8]{0:T(128)} %cnt_h.1, s32[16,1024]{1,0:T(8,128)} %bitcast.9, f32[16,1024]{1,0:T(8,128)} %bitcast.10, ...), custom_call_target="tpu_custom_call" | custom-call | tf_op jit(solution)/shard_map/gcn_step/pallas_call | solution.py:416
  46.6 0.9 %gcn_results.1 = (f32[1,1]{1,0:T(1,128)}, f32[602,256]{1,0:T(8,128)}, f32[41,256]{1,0:T(8,128)}) custom-call(f32[2,4,168,128]{3,2,1,0:T(8,128)S(1)} %get-tuple-element.8.outs, f32[8,128]{1,0:T(8,128)S(1)} %get-tuple-element.9.count_ref), custom_call_target="tpu_custom_call" | custom-call | tf_op jit(solution)/shard_map/gcn_results/pallas_call | solution.py:419
